TPU v7x, 256 devices: a whole 4x4x8 slice. The times are simulated.
256 devices in a mesh: grp: 4 (over y), gx: 16 (over z_hi, x, core), gy: 4 (over z_lo).
Axes of the slice: x: 4, y: 4, z: 8 (z_hi: 2, z_lo: 4; z = z_hi * 4 + z_lo), core: 2. Of those that a mesh axis runs over, the one named last changes fastest.
Arguments:
- velocity: float32 [3, 256, 32, 128], P(None, ('grp', 'gx'), 'gy'), may hold values from -12 to 12
- first_weight: bfloat16 [3, 3, 3, 64, 9], replicated, may hold values from -0.375 to 0.375
- first_bias: float32 [64], replicated, may hold values from -3 to 3
- second_weight: bfloat16 [3, 3, 3, 64, 64], replicated, may hold values from -0.15625 to 0.15625
- second_bias: float32 [64], replicated, may hold values from -3 to 3
- third_weight: bfloat16 [3, 3, 3, 64, 64], replicated, may hold values from -0.15625 to 0.15625
- third_bias: float32 [64], replicated, may hold values from -3 to 3
- last_weight: bfloat16 [3, 3, 3, 6, 64], replicated, may hold values from -0.15625 to 0.15625
Outputs:
- updated: float32 [3, 256, 32, 128], P(None, ('grp', 'gx'), 'gy')
- stress: float32 [6, 256, 32, 128], P(None, ('grp', 'gx'), 'gy')
All inputs are finite; a program needn't handle non-finite values.
Results may differ from a plain program's by a relative error of at most 0.002.
The roundings to bfloat16 on the way count: a program that leaves them out, or rounds other values in their place, can miss the bound.
Values may be sent and summed in bfloat16 or wider, within the bound.
A program may use at most 192 MiB of HBM per device.

v0:
```python
import functools

import jax
import jax.numpy as jnp
from jax import lax
from jax.experimental import pallas as pl
from jax.experimental.pallas import tpu as pltpu
from jax.sharding import PartitionSpec as P

MESH = pl.DeviceIdType.MESH
HALO = 6
NX, NY, NZ = 4, 8, 128
VX, VY = NX + 2 * HALO, NY + 2 * HALO
CH = 64
time_step = 0.1
viscosity = 0.05
power_input = 5.0
pairing = ((0, 3, 4), (3, 1, 5), (4, 5, 2))


def halo_copies():
    found = []
    for a in (1, -1, 2, -2, 0):
        for b in (0, 1, -1):
            if (a, b) == (0, 0):
                continue
            x0, y0 = HALO - NX * a, HALO - NY * b
            xl, xh = max(x0, 0), min(x0 + NX, VX)
            yl, yh = max(y0, 0), min(y0 + NY, VY)
            found.append((a, b, xl - x0, xl, xh - xl, yl - y0, yl, yh - yl))
    return found


def exchange_kernel(sizes, v_ref, vrow_ref, ext, total, own, e1, e2, local_sem, send, recv, s1, r1, s2, r2):
    groups, gxs, gys = sizes
    near = gxs // 2
    count_x = groups * gxs
    grp, gx, gy = lax.axis_index("grp"), lax.axis_index("gx"), lax.axis_index("gy")
    xi = grp * gxs + gx
    fetches = [
        pltpu.make_async_copy(
            vrow_ref.at[c], ext.at[pl.ds(HALO, NX), pl.ds(HALO, NY), c], local_sem.at[c]
        )
        for c in range(3)
    ]
    fetches.append(pltpu.make_async_copy(v_ref, own, local_sem.at[3]))
    for fetch in fetches:
        fetch.start()

    def at_offset(a, b):
        x = lax.rem(xi + a + count_x, count_x)
        return (x // gxs, lax.rem(x, gxs), lax.rem(gy + b + gys, gys))

    p = lax.rem(gx, near)
    q = (grp * 2 + gx // near) * gys + gy
    wide = groups * 2 * gys

    def first_peer(j):
        return (grp, (gx // near) * near + lax.rem(p + j, near), gy)

    def second_peer(j):
        t = lax.rem(q + j, wide)
        u = t // gys
        return (u // 2, lax.rem(u, 2) * near + p, lax.rem(t, gys))

    copies = halo_copies()
    barrier = pltpu.get_barrier_semaphore()
    peers = [at_offset(k[0], k[1]) for k in copies]
    firsts = [first_peer(j) for j in range(1, near)]
    seconds = [second_peer(j) for j in range(1, wide)]
    for peer in peers + firsts + seconds:
        pl.semaphore_signal(barrier, inc=1, device_id=peer, device_id_type=MESH)
    for fetch in fetches:
        fetch.wait()
    v = own[...]
    part = jnp.sum(jnp.sum(jnp.sum(0.5 * v * v, axis=0), axis=0), axis=0, keepdims=True)
    e1[0] = part
    pl.semaphore_wait(barrier, len(peers) + len(firsts) + len(seconds))

    started = []
    for k, (a, b, sx, dx, nx, sy, dy, ny) in enumerate(copies):
        copy = pltpu.make_async_remote_copy(
            src_ref=ext.at[pl.ds(HALO + sx, nx), pl.ds(HALO + sy, ny)],
            dst_ref=ext.at[pl.ds(dx, nx), pl.ds(dy, ny)],
            send_sem=send.at[k],
            recv_sem=recv.at[k],
            device_id=peers[k],
            device_id_type=MESH,
        )
        copy.start()
        started.append(copy)
    ones = []
    for j in range(1, near):
        copy = pltpu.make_async_remote_copy(
            src_ref=e1.at[0], dst_ref=e1.at[j], send_sem=s1.at[j], recv_sem=r1.at[j],
            device_id=firsts[j - 1], device_id_type=MESH,
        )
        copy.start()
        ones.append(copy)
    for copy in ones:
        copy.wait_recv()
    e2[0] = jnp.sum(e1[...], axis=0)
    twos = []
    for j in range(1, wide):
        copy = pltpu.make_async_remote_copy(
            src_ref=e2.at[0], dst_ref=e2.at[j], send_sem=s2.at[j], recv_sem=r2.at[j],
            device_id=seconds[j - 1], device_id_type=MESH,
        )
        copy.start()
        twos.append(copy)
    for copy in twos:
        copy.wait_recv()
    total[...] = jnp.sum(e2[...], axis=0)
    for copy in started:
        copy.wait_recv()
    for copy in started + ones + twos:
        copy.wait_send()


def exchange(sizes, velocity):
    groups, gxs, gys = sizes
    near, wide = gxs // 2, groups * 2 * gys
    n = len(halo_copies())
    return pl.pallas_call(
        functools.partial(exchange_kernel, sizes),
        out_shape=(
            jax.ShapeDtypeStruct((VX, VY, 3, 1, NZ), jnp.float32),
            jax.ShapeDtypeStruct((1, NZ), jnp.float32),
        ),
        in_specs=[pl.BlockSpec(memory_space=pl.ANY)] * 2,
        out_specs=(pl.BlockSpec(memory_space=pltpu.VMEM), pl.BlockSpec(memory_space=pltpu.VMEM)),
        scratch_shapes=[
            pltpu.VMEM((3, NX, NY, NZ), jnp.float32),
            pltpu.VMEM((near, 1, NZ), jnp.float32),
            pltpu.VMEM((wide, 1, NZ), jnp.float32),
            pltpu.SemaphoreType.DMA((4,)),
            pltpu.SemaphoreType.DMA((n,)),
            pltpu.SemaphoreType.DMA((n,)),
            pltpu.SemaphoreType.DMA((near,)),
            pltpu.SemaphoreType.DMA((near,)),
            pltpu.SemaphoreType.DMA((wide,)),
            pltpu.SemaphoreType.DMA((wide,)),
        ],
        compiler_params=pltpu.CompilerParams(collective_id=0, has_side_effects=True),
        name="exchange",
    )(velocity, velocity.reshape(3, NX, NY, 1, NZ))


def lanes_up(a):
    return pltpu.roll(a, 1, 1)


def lanes_down(a):
    return pltpu.roll(a, NZ - 1, 1)


def build_features(v, feats):
    fx, fy = VX - 2, VY - 2
    row = lax.broadcasted_iota(jnp.int32, (8, NZ), 0) < 3

    def one_x(x, carry):
        for y in range(fy):
            col = (x + 1) * VY + y + 1
            mid = v[pl.ds(col * 3, 8), :]
            if y == fy - 1:
                ahead = pltpu.roll(v[pl.ds((col + VY) * 3 - 2, 8), :], 6, 0)
            else:
                ahead = v[pl.ds((col + VY) * 3, 8), :]
            behind = v[pl.ds((col - VY) * 3, 8), :]
            below = v[pl.ds((col - 2) * 3, 8), :]
            first = jnp.where(row, ahead - behind, mid - below) * 0.5
            second = jnp.where(row, lanes_down(mid) - lanes_up(mid), 0.0) * 0.5
            both = jnp.concatenate([first, second], axis=0).astype(jnp.bfloat16)
            feats[pl.ds(pl.multiple_of((x * fy + y) * 16, 16), 16), :] = both
        return carry

    lax.fori_loop(0, fx, one_x, 0)


def conv(source, width, weight, out_x, out_y, emit):
    in_y = out_y + 2

    def one_x(x, carry):
        for y in range(0, out_y, 2):
            summed = None
            for dx in range(3):
                base = pl.multiple_of(((x + dx) * in_y + y) * width, width)
                window = jnp.concatenate(
                    [source[pl.ds(base, 3 * width), :], source[pl.ds(base + width, 3 * width), :]],
                    axis=1,
                )
                term = jnp.dot(weight[dx], window, preferred_element_type=jnp.float32)
                summed = term if summed is None else summed + term
            emit(x, y, summed[:, :NZ])
            emit(x, y + 1, summed[:, NZ:])
        return carry

    lax.fori_loop(0, out_x, one_x, 0)


def hidden_emit(target, bias, out_y):
    def emit(x, y, summed):
        value = lanes_up(summed[:CH]) + summed[CH : 2 * CH] + lanes_down(summed[2 * CH :]) + bias[...]
        base = pl.multiple_of((x * out_y + y) * CH, CH)
        target[pl.ds(base, CH), :] = jnp.tanh(value).astype(jnp.bfloat16)

    return emit


def compute_kernel(
    v, total, w1, b1, w2, b2, w3, b3, w4, updated, stress_out,
    feats, h1, h2, h3, st, wp1, wp2, wp3, wp4, c1, c2, c3, cells,
):
    eye = lax.broadcasted_iota(jnp.int32, (CH, CH), 0) == lax.broadcasted_iota(jnp.int32, (CH, CH), 1)
    for bias, held in ((b1, c1), (b2, c2), (b3, c3)):
        column = jnp.sum(jnp.where(eye, bias[...], 0.0), axis=1, keepdims=True)
        held[...] = jnp.broadcast_to(column, (CH, NZ))
    for w, wp in ((w2, wp2), (w3, wp3)):
        for dx in range(3):
            for dz in range(3):
                for dy in range(3):
                    tap = (dx * 3 + dy) * 3 + dz
                    wp[dx, dz * CH : (dz + 1) * CH, dy * CH : (dy + 1) * CH] = w[tap * CH : (tap + 1) * CH, :]
    channel = lax.broadcasted_iota(jnp.int32, (9, 48), 0)
    lane = lax.broadcasted_iota(jnp.int32, (9, 48), 1)
    kind = channel % 3
    slot = channel // 3 + jnp.where(kind == 2, 8, kind * 3)
    for dx in range(3):
        for dz in range(3):
            placed = None
            for dy in range(3):
                tap = (dx * 3 + dy) * 3 + dz
                spot = (lane == slot + dy * 16).astype(jnp.bfloat16)
                term = jnp.dot(w1[tap * CH : (tap + 1) * CH, :], spot, preferred_element_type=jnp.float32)
                placed = term if placed is None else placed + term
            wp1[dx, dz * CH : (dz + 1) * CH, :] = placed.astype(jnp.bfloat16)
    blank = jnp.zeros((2, CH), jnp.float32)
    for dx in range(3):
        for dy in range(3):
            rows = []
            for dz in range(3):
                tap = (dx * 3 + dy) * 3 + dz
                rows += [w4[tap].astype(jnp.float32), blank]
            rows.append(jnp.zeros((8, CH), jnp.float32))
            wp4[dx, :, dy * CH : (dy + 1) * CH] = jnp.concatenate(rows, axis=0).astype(jnp.bfloat16)

    build_features(v, feats)
    conv(feats, 16, wp1, VX - 4, VY - 4, hidden_emit(h1, c1, VY - 4))
    conv(h1, CH, wp2, VX - 6, VY - 6, hidden_emit(h2, c2, VY - 6))
    conv(h2, CH, wp3, VX - 8, VY - 8, hidden_emit(h3, c3, VY - 8))
    sy = VY - 10

    def stress_emit(x, y, summed):
        value = lanes_up(summed[:8]) + summed[8:16] + lanes_down(summed[16:24])
        st[pl.ds(pl.multiple_of((x * sy + y) * 8, 8), 8), :] = value

    conv(h3, CH, wp4, VX - 10, sy, stress_emit)

    energy = jnp.sum(total[...], axis=1, keepdims=True) / cells
    forcing = power_input / (2.0 * energy + 1e-06)
    for x in range(NX):
        def tau(k, ox, oy):
            return st[pl.ds(((x + 1 + ox) * sy + 1 + oy) * 8 + k, NY, stride=8), :]

        def vel(k, ox, oy):
            return v[pl.ds(((x + HALO + ox) * VY + HALO + oy) * 3 + k, NY, stride=3), :]

        here = [vel(k, 0, 0) for k in range(3)]
        for k in range(6):
            stress_out[k, x] = tau(k, 0, 0)
        for i in range(3):
            k0, k1, k2 = pairing[i]
            mid = tau(k2, 0, 0)
            div = (tau(k0, 1, 0) - tau(k0, -1, 0)) * 0.5 + (tau(k1, 0, 1) - tau(k1, 0, -1)) * 0.5
            div = div + (lanes_down(mid) - lanes_up(mid)) * 0.5
            xp, xm, yp, ym = vel(i, 1, 0), vel(i, -1, 0), vel(i, 0, 1), vel(i, 0, -1)
            zp, zm = lanes_down(here[i]), lanes_up(here[i])
            lap = (xp + xm + yp + ym + zm + zp) - 6.0 * here[i]
            advect = (xp - xm) * 0.5 * here[0] + (yp - ym) * 0.5 * here[1] + (zp - zm) * 0.5 * here[2]
            tendency = viscosity * lap - advect - div + forcing * here[i]
            updated[i, x] = here[i] + time_step * tendency


def compute(cells, v, total, w1, b1, w2, b2, w3, b3, w4):
    spec = pl.BlockSpec(memory_space=pltpu.VMEM)
    bf, f32 = jnp.bfloat16, jnp.float32
    return pl.pallas_call(
        lambda *refs: compute_kernel(*refs, cells),
        out_shape=(
            jax.ShapeDtypeStruct((3, NX, NY, NZ), f32),
            jax.ShapeDtypeStruct((6, NX, NY, NZ), f32),
        ),
        in_specs=[spec] * 9,
        out_specs=(spec, spec),
        scratch_shapes=[
            pltpu.VMEM(((VX - 2) * (VY - 2) * 16, NZ), bf),
            pltpu.VMEM(((VX - 4) * (VY - 4) * CH, NZ), bf),
            pltpu.VMEM(((VX - 6) * (VY - 6) * CH, NZ), bf),
            pltpu.VMEM(((VX - 8) * (VY - 8) * CH, NZ), bf),
            pltpu.VMEM(((VX - 10) * (VY - 10) * 8, NZ), f32),
            pltpu.VMEM((3, 3 * CH, 48), bf),
            pltpu.VMEM((3, 3 * CH, 3 * CH), bf),
            pltpu.VMEM((3, 3 * CH, 3 * CH), bf),
            pltpu.VMEM((3, 32, 3 * CH), bf),
            pltpu.VMEM((CH, NZ), f32),
            pltpu.VMEM((CH, NZ), f32),
            pltpu.VMEM((CH, NZ), f32),
        ],
        compiler_params=pltpu.CompilerParams(vmem_limit_bytes=56 << 20),
        name="evolve",
    )(
        v, total,
        w1.reshape(27 * CH, 9), b1.reshape(1, CH),
        w2.reshape(27 * CH, CH), b2.reshape(1, CH),
        w3.reshape(27 * CH, CH), b3.reshape(1, CH),
        w4.reshape(27, 6, CH),
    )


def solution(mesh):
    sizes = (mesh.shape["grp"], mesh.shape["gx"], mesh.shape["gy"])
    cells = float(NX * NY * NZ * sizes[0] * sizes[1] * sizes[2])

    def local(velocity, *weights):
        ext, total = exchange(sizes, velocity)
        return compute(cells, ext.reshape(VX * VY * 3, NZ), total, *weights)

    block = P(None, ("grp", "gx"), "gy", None)
    return jax.shard_map(
        local,
        mesh=mesh,
        in_specs=(block,) + (P(),) * 7,
        out_specs=(block, block),
        check_vma=False,
    )
```

profile of v0, /device:TPU:1, one launch (start us, length us, event | category | flops | bytes accessed | tf_op | source)
XLA Modules:
  0.0 58.4 jit_solution(1477321554766929287)
XLA Ops:
  0.6 1.9 %copy.10 = bf16[3,3,3,64,9]{4,3,2,1,0:T(8,128)(2,1)} copy(bf16[3,3,3,64,9]{3,2,4,1,0:T(4,128)(2,1)} %param.9) | data formatting | bytes 62208 | tf_op args[1]
  2.5 25.1 %exchange.1 = (f32[16,20,3,1,128]{4,3,2,1,0:T(1,128)}, f32[1,128]{1,0:T(1,128)}) custom-call(f32[3,4,8,128]{3,2,1,0:T(8,128)} %v_ref.1, f32[3,4,8,1,128]{4,3,2,1,0:T(1,128)} %bitcast.13), custom_call_target="tpu_custom_call" | custom-call | tf_op jit(solution)/shard_map/exchange/pallas_call | solution.py:124
  27.7 30.7 %evolve.1 = (f32[3,4,8,128]{3,2,1,0:T(8,128)}, f32[6,4,8,128]{3,2,1,0:T(8,128)}) custom-call(f32[960,128]{1,0:T(8,128)} %bitcast.10, f32[1,128]{1,0:T(1,128)} %get-tuple-element.5.refs_1_, bf16[1728,9]{1,0:T(8,128)(2,1)} %bitcast.9, f32[1,64]{1,0:T(1,128)} %bitcast.15, bf16[1728,64]{1,0:T(8,128)(2,1)} %bitcast.11, f32[1,64]{1,0:T(1,128)} %bitcast.16, ...), custom_call_target="tpu_custom_call" | custom-call | tf_op jit(solution)/shard_map/evolve/pallas_call | solution.py:287
where the time goes:
time: 58.6 us; the launch traced here: 58.4 us
  Pallas kernels  55.9 us (95%)
  local copies, waits for them, and re-layouts  1.91 us (3%)
  between operations  0.64 us (1%)
    pallas_call x1, Pallas kernels, compute(): pl.pallas_call(lambda *refs: compute_kernel(*refs, cells), out_shape=(jax...  30.7 us
    pallas_call x1, Pallas kernels, exchange(): pl.pallas_call(functools.partial(exchange_kernel, sizes), out_shape=(jax....  25.1 us
    unnamed x1, local copies, waits for them, and re-layouts  1.91 us

commit v1 on v0

v1 whole, which is shorter than its diff:
```python
import jax
import jax.numpy as jnp
from jax import lax
from jax.experimental import pallas as pl
from jax.experimental.pallas import tpu as pltpu
from jax.sharding import PartitionSpec as P

MESH = pl.DeviceIdType.MESH
HALO = 6
NX, NY, NZ = 4, 8, 128
VX, VY = NX + 2 * HALO, NY + 2 * HALO
CH = 64
time_step = 0.1
viscosity = 0.05
power_input = 5.0
pairing = ((0, 3, 4), (3, 1, 5), (4, 5, 2))


def halo_copies():
    found = []
    order = [(a, b) for s in (1, -1) for a in (s, 2 * s) for b in (0, 1, -1)] + [(0, 1), (0, -1)]
    for a, b in order:
        x0, y0 = HALO - NX * a, HALO - NY * b
        xl, xh = max(x0, 0), min(x0 + NX, VX)
        yl, yh = max(y0, 0), min(y0 + NY, VY)
        found.append((a, b, xl - x0, xl, xh - xl, yl - y0, yl, yh - yl))
    return found


def lanes_up(a):
    return pltpu.roll(a, 1, 1)


def lanes_down(a):
    return pltpu.roll(a, NZ - 1, 1)


def place(r, side, halo):
    return halo + r + side * (3 - 2 * r)


def build_features(v, feats, side, low, count):
    fy = VY - 2
    row = lax.broadcasted_iota(jnp.int32, (8, NZ), 0) < 3

    def one_x(i, carry):
        x = place(low + i, side, HALO - 1)
        for y in range(fy):
            col = (x + 1) * VY + y + 1
            mid = v[pl.ds(col * 3, 8), :]
            if y == fy - 1:
                ahead = pltpu.roll(v[pl.ds((col + VY) * 3 - 2, 8), :], 6, 0)
            else:
                ahead = v[pl.ds((col + VY) * 3, 8), :]
            behind = v[pl.ds((col - VY) * 3, 8), :]
            below = v[pl.ds((col - 2) * 3, 8), :]
            first = jnp.where(row, ahead - behind, mid - below) * 0.5
            second = jnp.where(row, lanes_down(mid) - lanes_up(mid), 0.0) * 0.5
            both = jnp.concatenate([first, second], axis=0).astype(jnp.bfloat16)
            feats[pl.ds(pl.multiple_of((x * fy + y) * 16, 16), 16), :] = both
        return carry

    lax.fori_loop(0, count, one_x, 0)


def conv(source, width, weight, halo, side, low, count, emit):
    out_y = NY + 2 * halo
    in_y = out_y + 2

    def rows_of(i, carry):
        for half in range(2):
            x = place(low + 2 * i + half, side, halo)
            for y in range(0, out_y, 2):
                parts = []
                for dx in range(3):
                    base = pl.multiple_of(((x + dx) * in_y + y) * width, width)
                    parts.append(
                        jnp.concatenate(
                            [source[pl.ds(base, 3 * width), :], source[pl.ds(base + width, 3 * width), :]],
                            axis=1,
                        )
                    )
                if width == 16:
                    summed = jnp.dot(weight[...], jnp.concatenate(parts, axis=0), preferred_element_type=jnp.float32)
                else:
                    summed = None
                    for dx in range(3):
                        term = jnp.dot(weight[dx], parts[dx], preferred_element_type=jnp.float32)
                        summed = term if summed is None else summed + term
                emit(x, y, summed[:, :NZ])
                emit(x, y + 1, summed[:, NZ:])
        return carry

    lax.fori_loop(0, count // 2, rows_of, 0)


def hidden_emit(target, bias, halo):
    out_y = NY + 2 * halo

    def emit(x, y, summed):
        value = lanes_up(summed[:CH]) + summed[CH : 2 * CH] + lanes_down(summed[2 * CH :]) + bias[...]
        base = pl.multiple_of((x * out_y + y) * CH, CH)
        target[pl.ds(base, CH), :] = jnp.tanh(value).astype(jnp.bfloat16)

    return emit


def prepare_biases(b, held):
    eye = lax.broadcasted_iota(jnp.int32, (CH, CH), 0) == lax.broadcasted_iota(jnp.int32, (CH, CH), 1)
    for bias, out in zip(b, held):
        column = jnp.sum(jnp.where(eye, bias[...], 0.0), axis=1, keepdims=True)
        out[...] = jnp.broadcast_to(column, (CH, NZ))


def prepare_hidden(w, wp):
    for dx in range(3):
        for dz in range(3):
            for dy in range(3):
                tap = (dx * 3 + dy) * 3 + dz
                wp[dx, dz * CH : (dz + 1) * CH, dy * CH : (dy + 1) * CH] = w[tap * CH : (tap + 1) * CH, :]


def prepare_first(w1, wp1):
    channel = lax.broadcasted_iota(jnp.int32, (9, 144), 0)
    lane = lax.broadcasted_iota(jnp.int32, (9, 144), 1)
    kind = channel % 3
    slot = channel // 3 + jnp.where(kind == 2, 8, kind * 3)
    for dz in range(3):
        placed = None
        for dx in range(3):
            for dy in range(3):
                tap = (dx * 3 + dy) * 3 + dz
                spot = (lane == slot + (dx * 3 + dy) * 16).astype(jnp.bfloat16)
                term = jnp.dot(w1[tap * CH : (tap + 1) * CH, :], spot, preferred_element_type=jnp.float32)
                placed = term if placed is None else placed + term
        wp1[dz * CH : (dz + 1) * CH, :] = placed.astype(jnp.bfloat16)


def prepare_last(w4, wp4):
    blank = jnp.zeros((2, CH), jnp.float32)
    for dx in range(3):
        for dy in range(3):
            rows = []
            for dz in range(3):
                tap = (dx * 3 + dy) * 3 + dz
                rows += [w4[tap].astype(jnp.float32), blank]
            rows.append(jnp.zeros((8, CH), jnp.float32))
            wp4[dx, :, dy * CH : (dy + 1) * CH] = jnp.concatenate(rows, axis=0).astype(jnp.bfloat16)


def finish(v, st, total, cells, updated, stress_out):
    sy = NY + 2
    energy = jnp.sum(total, axis=1, keepdims=True) / cells
    forcing = power_input / (2.0 * energy + 1e-06)
    for x in range(NX):
        def tau(k, ox, oy):
            return st[pl.ds(((x + 1 + ox) * sy + 1 + oy) * 8 + k, NY, stride=8), :]

        def vel(k, ox, oy):
            return v[pl.ds(((x + HALO + ox) * VY + HALO + oy) * 3 + k, NY, stride=3), :]

        here = [vel(k, 0, 0) for k in range(3)]
        for k in range(6):
            stress_out[k, x] = tau(k, 0, 0)
        for i in range(3):
            k0, k1, k2 = pairing[i]
            mid = tau(k2, 0, 0)
            div = (tau(k0, 1, 0) - tau(k0, -1, 0)) * 0.5 + (tau(k1, 0, 1) - tau(k1, 0, -1)) * 0.5
            div = div + (lanes_down(mid) - lanes_up(mid)) * 0.5
            xp, xm, yp, ym = vel(i, 1, 0), vel(i, -1, 0), vel(i, 0, 1), vel(i, 0, -1)
            zp, zm = lanes_down(here[i]), lanes_up(here[i])
            lap = (xp + xm + yp + ym + zm + zp) - 6.0 * here[i]
            advect = (xp - xm) * 0.5 * here[0] + (yp - ym) * 0.5 * here[1] + (zp - zm) * 0.5 * here[2]
            tendency = viscosity * lap - advect - div + forcing * here[i]
            updated[i, x] = here[i] + time_step * tendency


def step_kernel(
    sizes, v_ref, vrow_ref, w1_hbm, b1_hbm, w2_hbm, b2_hbm, w3_hbm, b3_hbm, w4_hbm, updated, stress_out,
    ext, own, e1, e2, w1, b1, w2, b2, w3, b3, w4,
    feats, h1, h2, h3, st, wp1, wp2, wp3, wp4, c1, c2, c3,
    local_sem, weight_sem, send, recv, s1, r1, s2, r2,
):
    groups, gxs, gys = sizes
    near = gxs // 2
    count_x = groups * gxs
    cells = float(NX * NY * NZ * count_x * gys)
    grp, gx, gy = lax.axis_index("grp"), lax.axis_index("gx"), lax.axis_index("gy")
    xi = grp * gxs + gx
    p = lax.rem(gx, near)
    q = (grp * 2 + gx // near) * gys + gy
    wide = groups * 2 * gys
    side = p // (near // 2)

    def at_offset(a, b):
        x = lax.rem(xi + a + count_x, count_x)
        return (x // gxs, lax.rem(x, gxs), lax.rem(gy + b + gys, gys))

    def first_peer(j):
        return (grp, (gx // near) * near + lax.rem(p + j, near), gy)

    def second_peer(j):
        t = lax.rem(q + j, wide)
        u = t // gys
        return (u // 2, lax.rem(u, 2) * near + p, lax.rem(t, gys))

    copies = halo_copies()
    peers = [at_offset(k[0], k[1]) for k in copies]
    firsts = [first_peer(j) for j in range(1, near)]
    seconds = [second_peer(j) for j in range(1, wide)]
    barrier = pltpu.get_barrier_semaphore()
    for peer in peers + firsts + seconds:
        pl.semaphore_signal(barrier, inc=1, device_id=peer, device_id_type=MESH)

    fetches = [
        pltpu.make_async_copy(vrow_ref.at[c], ext.at[pl.ds(HALO, NX), pl.ds(HALO, NY), c], local_sem.at[c])
        for c in range(3)
    ]
    fetches.append(pltpu.make_async_copy(v_ref, own, local_sem.at[3]))
    pairs = ((w1_hbm, w1), (b1_hbm, b1), (w2_hbm, w2), (b2_hbm, b2), (w3_hbm, w3), (b3_hbm, b3), (w4_hbm, w4))
    loads = [pltpu.make_async_copy(a, b, weight_sem.at[k]) for k, (a, b) in enumerate(pairs)]
    for fetch in fetches + loads:
        fetch.start()
    for fetch in fetches:
        fetch.wait()
    square = own[...]
    e1[0] = jnp.sum(jnp.sum(jnp.sum(0.5 * square * square, axis=0), axis=0), axis=0, keepdims=True)
    for load in loads:
        load.wait()
    prepare_biases((b1, b2, b3), (c1, c2, c3))
    prepare_first(w1, wp1)
    prepare_hidden(w2, wp2)
    prepare_hidden(w3, wp3)
    prepare_last(w4, wp4)
    pl.semaphore_wait(barrier, len(peers) + len(firsts) + len(seconds))

    started = []
    for k, (a, b, sx, dx, nx, sy, dy, ny) in enumerate(copies):
        copy = pltpu.make_async_remote_copy(
            src_ref=ext.at[pl.ds(HALO + sx, nx), pl.ds(HALO + sy, ny)],
            dst_ref=ext.at[pl.ds(dx, nx), pl.ds(dy, ny)],
            send_sem=send.at[k],
            recv_sem=recv.at[k],
            device_id=peers[k],
            device_id_type=MESH,
        )
        copy.start()
        started.append(copy)
    ones = []
    for j in range(1, near):
        copy = pltpu.make_async_remote_copy(
            src_ref=e1.at[0], dst_ref=e1.at[j], send_sem=s1.at[j], recv_sem=r1.at[j],
            device_id=firsts[j - 1], device_id_type=MESH,
        )
        copy.start()
        ones.append(copy)

    def arrive(k):
        index = k if k >= 12 else k % 6 + 6 * (side if k < 6 else 1 - side)
        pltpu.make_async_remote_copy(
            src_ref=ext.at[pl.ds(HALO, copies[k][4]), pl.ds(HALO, copies[k][7])],
            dst_ref=ext.at[pl.ds(HALO, copies[k][4]), pl.ds(HALO, copies[k][7])],
            send_sem=send.at[k],
            recv_sem=recv.at[index],
            device_id=peers[k],
            device_id_type=MESH,
        ).wait_recv()

    for k in range(6, 14):
        arrive(k)
    v = ext.reshape(VX * VY * 3, NZ)
    emit1, emit2, emit3 = hidden_emit(h1, c1, 4), hidden_emit(h2, c2, 3), hidden_emit(h3, c3, 2)

    def stress_emit(x, y, summed):
        value = lanes_up(summed[:8]) + summed[8:16] + lanes_down(summed[16:24])
        st[pl.ds(pl.multiple_of((x * (NY + 2) + y) * 8, 8), 8), :] = value

    build_features(v, feats, side, 1, 8)
    for copy in ones:
        copy.wait_recv()
    e2[0] = jnp.sum(e1[...], axis=0)
    conv(feats, 16, wp1, 4, side, 2, 6, emit1)
    twos = []
    for j in range(1, wide):
        copy = pltpu.make_async_remote_copy(
            src_ref=e2.at[0], dst_ref=e2.at[j], send_sem=s2.at[j], recv_sem=r2.at[j],
            device_id=seconds[j - 1], device_id_type=MESH,
        )
        copy.start()
        twos.append(copy)
    conv(h1, CH, wp2, 3, side, 3, 4, emit2)
    conv(h2, CH, wp3, 2, side, 4, 2, emit3)
    for k in range(6):
        arrive(k)
    build_features(v, feats, side, -5, 6)
    conv(feats, 16, wp1, 4, side, -4, 6, emit1)
    conv(h1, CH, wp2, 3, side, -3, 6, emit2)
    conv(h2, CH, wp3, 2, side, -2, 6, emit3)
    conv(h3, CH, wp4, 1, side, -1, 6, stress_emit)
    for copy in twos:
        copy.wait_recv()
    finish(v, st, jnp.sum(e2[...], axis=0), cells, updated, stress_out)
    for copy in started + ones + twos:
        copy.wait_send()


def solution(mesh):
    sizes = (mesh.shape["grp"], mesh.shape["gx"], mesh.shape["gy"])
    near, wide = sizes[1] // 2, sizes[0] * 2 * sizes[2]
    n = len(halo_copies())
    bf, f32 = jnp.bfloat16, jnp.float32

    def local(velocity, w1, b1, w2, b2, w3, b3, w4):
        spec = pl.BlockSpec(memory_space=pltpu.VMEM)
        dma = pltpu.SemaphoreType.DMA
        return pl.pallas_call(
            lambda *refs: step_kernel(sizes, *refs),
            out_shape=(
                jax.ShapeDtypeStruct((3, NX, NY, NZ), f32),
                jax.ShapeDtypeStruct((6, NX, NY, NZ), f32),
            ),
            in_specs=[pl.BlockSpec(memory_space=pl.ANY)] * 9,
            out_specs=(spec, spec),
            scratch_shapes=[
                pltpu.VMEM((VX, VY, 3, 1, NZ), f32),
                pltpu.VMEM((3, NX, NY, NZ), f32),
                pltpu.VMEM((near, 1, NZ), f32),
                pltpu.VMEM((wide, 1, NZ), f32),
                pltpu.VMEM((27 * CH, 9), bf),
                pltpu.VMEM((1, CH), f32),
                pltpu.VMEM((27 * CH, CH), bf),
                pltpu.VMEM((1, CH), f32),
                pltpu.VMEM((27 * CH, CH), bf),
                pltpu.VMEM((1, CH), f32),
                pltpu.VMEM((27, 6, CH), bf),
                pltpu.VMEM(((VX - 2) * (VY - 2) * 16, NZ), bf),
                pltpu.VMEM(((VX - 4) * (VY - 4) * CH, NZ), bf),
                pltpu.VMEM(((VX - 6) * (VY - 6) * CH, NZ), bf),
                pltpu.VMEM(((VX - 8) * (VY - 8) * CH, NZ), bf),
                pltpu.VMEM(((VX - 10) * (VY - 10) * 8, NZ), f32),
                pltpu.VMEM((3 * CH, 144), bf),
                pltpu.VMEM((3, 3 * CH, 3 * CH), bf),
                pltpu.VMEM((3, 3 * CH, 3 * CH), bf),
                pltpu.VMEM((3, 32, 3 * CH), bf),
                pltpu.VMEM((CH, NZ), f32),
                pltpu.VMEM((CH, NZ), f32),
                pltpu.VMEM((CH, NZ), f32),
                dma((4,)),
                dma((7,)),
                dma((n,)),
                dma((n,)),
                dma((near,)),
                dma((near,)),
                dma((wide,)),
                dma((wide,)),
            ],
            compiler_params=pltpu.CompilerParams(
                collective_id=0, has_side_effects=True, vmem_limit_bytes=56 << 20
            ),
            name="step",
        )(
            velocity, velocity.reshape(3, NX, NY, 1, NZ),
            w1.reshape(27 * CH, 9), b1.reshape(1, CH),
            w2.reshape(27 * CH, CH), b2.reshape(1, CH),
            w3.reshape(27 * CH, CH), b3.reshape(1, CH),
            w4.reshape(27, 6, CH),
        )

    block = P(None, ("grp", "gx"), "gy", None)
    return jax.shard_map(
        local,
        mesh=mesh,
        in_specs=(block,) + (P(),) * 7,
        out_specs=(block, block),
        check_vma=False,
    )
```

time: 58.6 us -> 48 us (0.82)
  Pallas kernels: 55.9 us -> 43.2 us
  local copies, waits for them, and re-layouts: 1.91 us -> 4 us
    pallas_call x2 -> x1, Pallas kernels: 55.9 us -> 43.2 us  [local(): pl.pallas_call(lambda *refs: step_kernel(sizes, *refs), out_shape=(jax.Sh...]
    unnamed x1 -> x5, local copies, waits for them, and re-layouts: 1.91 us -> 4 us
where the time goes in v1:
time: 48 us; the launch traced here: 47.9 us
  Pallas kernels  43.2 us (90%)
  local copies, waits for them, and re-layouts  4 us (8%)
  between operations  0.65 us (1%)
    pallas_call x1, Pallas kernels, local(): pl.pallas_call(lambda *refs: step_kernel(sizes, *refs), out_shape=(jax.Sh...  43.2 us
    unnamed x5, local copies, waits for them, and re-layouts  4 us

profile of v1, /device:TPU:1, one launch (start us, length us, event | category | flops | bytes accessed | tf_op | source)
XLA Modules:
  0.0 47.9 jit_solution(13669068577164328617)
XLA Ops:
  0.6 1.9 %copy.10 = bf16[3,3,3,64,9]{4,3,2,1,0:T(8,128)(2,1)} copy(bf16[3,3,3,64,9]{3,2,4,1,0:T(4,128)(2,1)} %param.9) | data formatting | bytes 62208 | tf_op args[1]
  2.5 43.2 %step.1 = (f32[3,4,8,128]{3,2,1,0:T(8,128)}, f32[6,4,8,128]{3,2,1,0:T(8,128)}) custom-call(f32[3,4,8,128]{3,2,1,0:T(8,128)} %refs_0_.1, f32[3,4,8,1,128]{4,3,2,1,0:T(1,128)} %bitcast.11, bf16[1728,9]{1,0:T(8,128)(2,1)} %bitcast.8, f32[1,64]{1,0:T(1,128)} %bitcast.13, bf16[1728,64]{1,0:T(8,128)(2,1)} %bitcast.9, f32[1,64]{1,0:T(1,128)} %bitcast.14, ...), custom_call_target="tpu_custom_call" | custom-call | tf_op jit(solution)/shard_map/step/pallas_call | solution.py:316
  45.8 0.0 copy-start
  45.8 1.5 %copy.13 = f32[3,4,8,128]{3,2,1,0:T(8,128)} copy(f32[3,4,8,128]{3,2,1,0:T(8,128)} %get-tuple-element.4) | data formatting | bytes 98304
  47.2 0.0 copy-done
  47.2 0.6 %copy.14 = f32[6,4,8,128]{3,2,1,0:T(8,128)} copy(f32[6,4,8,128]{3,2,1,0:T(8,128)S(1)} %copy-done) | data formatting | bytes 196608
Async XLA Ops:
  45.8 1.5 %copy-start = (f32[6,4,8,128]{3,2,1,0:T(8,128)S(1)}, f32[6,4,8,128]{3,2,1,0:T(8,128)}, u32[]{:S(2)}) copy-start(f32[6,4,8,128]{3,2,1,0:T(8,128)} %get-tuple-element.5) | copy-start | bytes 294916

commit v2 on v1

v2 whole, which is shorter than its diff:
```python
import jax
import jax.numpy as jnp
from jax import lax
from jax.experimental import pallas as pl
from jax.experimental.pallas import tpu as pltpu
from jax.sharding import PartitionSpec as P

MESH = pl.DeviceIdType.MESH
HALO = 6
NX, NY, NZ = 4, 8, 128
VX, VY = NX + 2 * HALO, NY + 2 * HALO
CH = 64
time_step = 0.1
viscosity = 0.05
power_input = 5.0
pairing = ((0, 3, 4), (3, 1, 5), (4, 5, 2))


def halo_copies():
    parts = []
    for b in (0, 1, -1):
        y0 = HALO - NY * b
        low, high = max(y0, 0), min(y0 + NY, VY)
        parts.append((b, low - y0, low, high - low))
    ranges = (("outer", 0), ("second", 0), ("beside", 1), ("partner", 0))
    return [(kind, *part) for kind, first in ranges for part in parts[first:]]


def halo_span(kind, side):
    if kind == "outer":
        return 2 * side - 1, HALO, HALO + NX - 2 * NX * side, NX
    if kind == "second":
        return 2 - 4 * side, HALO + 2 - 2 * side, HALO - 6 + 14 * side, 2
    if kind == "partner":
        return 1 - 2 * side, HALO + 2 - 2 * side, HALO - 2 + 6 * side, 2
    return 0, HALO, HALO, NX


def lanes_up(a):
    return pltpu.roll(a, 1, 1)


def lanes_down(a):
    return pltpu.roll(a, NZ - 1, 1)


def place(r, side, halo):
    return halo + r + side * (3 - 2 * r)


def build_features(v, feats, side, high, count):
    fy = VY - 2
    row = lax.broadcasted_iota(jnp.int32, (8, NZ), 0)

    def one_x(x):
        for y in range(fy):
            col = (x + 1) * VY + y + 1
            mid = v[pl.ds(col * 3, 8), :]
            if y == fy - 1:
                ahead = pltpu.roll(v[pl.ds((col + VY) * 3 - 2, 8), :], 6, 0)
            else:
                ahead = v[pl.ds((col + VY) * 3, 8), :]
            behind = v[pl.ds((col - VY) * 3, 8), :]
            below = v[pl.ds((col - 2) * 3, 8), :]
            again = v[pl.ds((col - 1) * 3, 8), :]
            held = jnp.where(row < 3, mid, jnp.where(row < 6, again, below))
            along = (lanes_down(held) - lanes_up(held)) * 0.5
            shifted = lanes_up(along)
            across = jnp.where(row < 3, ahead - behind, mid - below) * 0.5
            across = jnp.where(row < 6, across, jnp.where(row == 6, pltpu.roll(shifted, 1, 0), 0.0))
            depth = jnp.where(row < 3, along, jnp.where(row < 6, lanes_down(along), shifted))
            base = pl.multiple_of((x * fy + y) * 32, 32)
            feats[pl.ds(base, 16), :] = jnp.concatenate([across, depth], axis=0).astype(jnp.bfloat16)
            beside = jnp.concatenate([lanes_down(across), lanes_up(across)], axis=0)
            feats[pl.ds(base + 16, 16), :] = beside.astype(jnp.bfloat16)

    def two_rows(i, carry):
        one_x(place(high - 2 * i, side, HALO - 1))
        one_x(place(high - 2 * i - 1, side, HALO - 1))
        return carry

    lax.fori_loop(0, count // 2, two_rows, 0)


def conv(source, taps, halo, side, high, count, emit):
    out_y = NY + 2 * halo

    def one_row(r):
        x = place(r, side, halo)
        for y in range(0, out_y, 2):
            emit(x, y, taps(source, x, y, out_y + 2))

    def two_rows(i, carry):
        one_row(high - 2 * i)
        one_row(high - 2 * i - 1)
        return carry

    lax.fori_loop(0, count // 2, two_rows, 0)
    if count % 2:
        one_row(high - count + 1)


def window(source, width, x, y, in_y, count):
    base = pl.multiple_of((x * in_y + y) * width, width)
    return source[pl.ds(base, count * width), :]


def beside(make):
    return jnp.concatenate([make(0), make(1)], axis=1)


def dot(a, b):
    return jnp.dot(a, b, preferred_element_type=jnp.float32)


def first_taps(weight):
    def taps(source, x, y, in_y):
        def column(j):
            return jnp.concatenate([window(source, 32, x + dx, y + j, in_y, 3) for dx in range(3)], axis=0)

        return dot(weight[...], beside(column))

    return taps


def wide_taps(weight):
    def taps(source, x, y, in_y):
        summed = None
        for dx in range(3):
            term = dot(weight[dx], beside(lambda j: window(source, CH, x + dx, y + j, in_y, 3)))
            summed = term if summed is None else summed + term
        return summed

    return taps


def store_hidden(target, x, y, out_y, value):
    base = pl.multiple_of((x * out_y + y) * CH, CH)
    target[pl.ds(base, CH), :] = jnp.tanh(value).astype(jnp.bfloat16)


def first_emit(target, bias, halo):
    def emit(x, y, summed):
        for j in range(2):
            value = summed[:, j * NZ : (j + 1) * NZ] + bias[...]
            store_hidden(target, x, y + j, NY + 2 * halo, value)

    return emit


def hidden_emit(target, bias, halo):
    def emit(x, y, summed):
        for j in range(2):
            part = summed[:, j * NZ : (j + 1) * NZ]
            value = lanes_up(part[:CH]) + (part[CH : 2 * CH] + bias[...]) + lanes_down(part[2 * CH :])
            store_hidden(target, x, y + j, NY + 2 * halo, value)

    return emit


def last_emit(st):
    def emit(x, y, summed):
        for j in range(2):
            part = summed[:, j * NZ : (j + 1) * NZ]
            value = lanes_up(part[:8]) + part[8:16] + lanes_down(part[16:24])
            st[pl.ds(pl.multiple_of((x * (NY + 2) + y + j) * 8, 8), 8), :] = value

    return emit


def prepare_biases(b, held):
    eye = lax.broadcasted_iota(jnp.int32, (CH, CH), 0) == lax.broadcasted_iota(jnp.int32, (CH, CH), 1)
    for bias, out in zip(b, held):
        column = jnp.sum(jnp.where(eye, bias[...], 0.0), axis=1, keepdims=True)
        out[...] = jnp.broadcast_to(column, (CH, NZ))


def prepare_hidden(w, wp):
    for dx in range(3):
        for dz in range(3):
            for dy in range(3):
                tap = (dx * 3 + dy) * 3 + dz
                wp[dx, dz * CH : (dz + 1) * CH, dy * CH : (dy + 1) * CH] = w[tap * CH : (tap + 1) * CH, :]


def prepare_first(w1, wp1):
    source = lax.broadcasted_iota(jnp.int32, (81, 288), 0)
    lane = lax.broadcasted_iota(jnp.int32, (81, 288), 1)
    tap, channel = source // 9, source % 9
    i, j = channel // 3, channel % 3
    pair = i + 3 * j
    slots = (
        jnp.where(j < 2, 24 + pair, jnp.where(i < 2, 14 + i, 6)),
        jnp.where(j < 2, pair, 8 + i),
        jnp.where(j < 2, 16 + pair, 11 + i),
    )
    held = w1[...].astype(jnp.float32)
    placed = None
    for dz in range(3):
        spot = (lane == tap * 32 + slots[dz]).astype(jnp.bfloat16)
        term = dot(held[:, dz, :].T.astype(jnp.bfloat16), spot)
        placed = term if placed is None else placed + term
    wp1[...] = placed.astype(jnp.bfloat16)


def prepare_last(w4, wp4):
    blank = jnp.zeros((2, CH), jnp.float32)
    for dx in range(3):
        for dy in range(3):
            rows = []
            for dz in range(3):
                tap = (dx * 3 + dy) * 3 + dz
                rows += [w4[tap].astype(jnp.float32), blank]
            rows.append(jnp.zeros((8, CH), jnp.float32))
            wp4[dx, :, dy * CH : (dy + 1) * CH] = jnp.concatenate(rows, axis=0).astype(jnp.bfloat16)


def finish(v, st, total, cells, updated, stress_out):
    sy = NY + 2
    energy = jnp.sum(total, axis=1, keepdims=True) / cells
    forcing = power_input / (2.0 * energy + 1e-06)
    for x in range(NX):
        def tau(k, ox, oy):
            return st[pl.ds(((x + 1 + ox) * sy + 1 + oy) * 8 + k, NY, stride=8), :]

        def vel(k, ox, oy):
            return v[pl.ds(((x + HALO + ox) * VY + HALO + oy) * 3 + k, NY, stride=3), :]

        here = [vel(k, 0, 0) for k in range(3)]
        for k in range(6):
            stress_out[k, x] = tau(k, 0, 0)
        for i in range(3):
            k0, k1, k2 = pairing[i]
            mid = tau(k2, 0, 0)
            div = (tau(k0, 1, 0) - tau(k0, -1, 0)) * 0.5 + (tau(k1, 0, 1) - tau(k1, 0, -1)) * 0.5
            div = div + (lanes_down(mid) - lanes_up(mid)) * 0.5
            xp, xm, yp, ym = vel(i, 1, 0), vel(i, -1, 0), vel(i, 0, 1), vel(i, 0, -1)
            zp, zm = lanes_down(here[i]), lanes_up(here[i])
            lap = (xp + xm + yp + ym + zm + zp) - 6.0 * here[i]
            advect = (xp - xm) * 0.5 * here[0] + (yp - ym) * 0.5 * here[1] + (zp - zm) * 0.5 * here[2]
            tendency = viscosity * lap - advect - div + forcing * here[i]
            updated[i, x] = here[i] + time_step * tendency


def step_kernel(
    sizes, v_ref, vrow_ref, w1_hbm, b1_hbm, w2_hbm, b2_hbm, w3_hbm, b3_hbm, w4_hbm, updated, stress_out,
    ext, own, e1, e2, w1, b1, w2, b2, w3, b3, w4,
    feats, h1, h2, h3, st, wp1, wp2, wp3, wp4, c1, c2, c3,
    local_sem, weight_sem, send, recv, s1, r1, s2, r2, s3, r3,
):
    groups, gxs, gys = sizes
    near = gxs // 2
    count_x = groups * gxs
    cells = float(NX * NY * NZ * count_x * gys)
    grp, gx, gy = lax.axis_index("grp"), lax.axis_index("gx"), lax.axis_index("gy")
    xi = grp * gxs + gx
    p = lax.rem(gx, near)
    q = (grp * 2 + gx // near) * gys + gy
    wide = groups * 2 * gys
    side = lax.rem(gx, 2)

    def at_offset(a, b):
        x = lax.rem(xi + a + count_x, count_x)
        return (x // gxs, lax.rem(x, gxs), lax.rem(gy + b + gys, gys))

    def first_peer(j):
        return (grp, (gx // near) * near + lax.rem(p + j, near), gy)

    def second_peer(j):
        t = lax.rem(q + j, wide)
        u = t // gys
        return (u // 2, lax.rem(u, 2) * near + p, lax.rem(t, gys))

    copies = halo_copies()
    peers = [at_offset(halo_span(k[0], side)[0], k[1]) for k in copies]
    givers = [at_offset(4 * side - 2, b) for b in (0, 1, -1)]
    firsts = [first_peer(j) for j in range(1, near)]
    seconds = [second_peer(j) for j in range(1, wide)]
    barrier = pltpu.get_barrier_semaphore()
    for peer in peers + givers + firsts + seconds:
        pl.semaphore_signal(barrier, inc=1, device_id=peer, device_id_type=MESH)

    fetches = [
        pltpu.make_async_copy(vrow_ref.at[c], ext.at[pl.ds(HALO, NX), pl.ds(HALO, NY), c], local_sem.at[c])
        for c in range(3)
    ]
    fetches.append(pltpu.make_async_copy(v_ref, own, local_sem.at[3]))
    pairs = ((w1_hbm, w1), (b1_hbm, b1), (w2_hbm, w2), (b2_hbm, b2), (w3_hbm, w3), (b3_hbm, b3), (w4_hbm, w4))
    loads = [pltpu.make_async_copy(a, b, weight_sem.at[k]) for k, (a, b) in enumerate(pairs)]
    for fetch in fetches + loads:
        fetch.start()
    for fetch in fetches:
        fetch.wait()
    pl.semaphore_wait(barrier, len(peers) + len(givers) + len(firsts) + len(seconds))

    started = []
    for k, (kind, b, sy, dy, ny) in enumerate(copies):
        _, sx, dx, nx = halo_span(kind, side)
        copy = pltpu.make_async_remote_copy(
            src_ref=ext.at[pl.ds(sx, nx), pl.ds(HALO + sy, ny)],
            dst_ref=ext.at[pl.ds(dx, nx), pl.ds(dy, ny)],
            send_sem=send.at[k],
            recv_sem=recv.at[k],
            device_id=peers[k],
            device_id_type=MESH,
        )
        copy.start()
        started.append(copy)

    square = own[...]
    e1[0] = jnp.sum(jnp.sum(jnp.sum(0.5 * square * square, axis=0), axis=0), axis=0, keepdims=True)
    for load in loads:
        load.wait()
    prepare_biases((b1, b2, b3), (c1, c2, c3))
    prepare_first(w1, wp1)
    prepare_hidden(w2, wp2)
    ones = []
    for j in range(1, near):
        copy = pltpu.make_async_remote_copy(
            src_ref=e1.at[0], dst_ref=e1.at[j], send_sem=s1.at[j], recv_sem=r1.at[j],
            device_id=firsts[j - 1], device_id_type=MESH,
        )
        copy.start()
        ones.append(copy)
    prepare_hidden(w3, wp3)
    prepare_last(w4, wp4)
    v = ext.reshape(VX * VY * 3, NZ)

    def one(high, count):
        conv(feats, first_taps(wp1), 4, side, high, count, first_emit(h1, c1, 4))

    def two(high, count):
        conv(h1, wide_taps(wp2), 3, side, high, count, hidden_emit(h2, c2, 3))

    def three(high, count):
        conv(h2, wide_taps(wp3), 2, side, high, count, hidden_emit(h3, c3, 2))

    def four(high, count):
        conv(h3, wide_taps(wp4), 1, side, high, count, last_emit(st))

    def share(slot, held, halo, width):
        rows = (NY + 2 * halo) * width
        copy = pltpu.make_async_remote_copy(
            src_ref=held.at[pl.ds(pl.multiple_of((halo + 3 - 3 * side) * rows, width), rows)],
            dst_ref=held.at[pl.ds(pl.multiple_of((halo - 1 + 5 * side) * rows, width), rows)],
            send_sem=s3.at[slot],
            recv_sem=r3.at[slot],
            device_id=peers[8],
            device_id_type=MESH,
        )
        copy.start()
        started.append(copy)
        return copy

    for copy in started[6:11]:
        copy.wait_recv()
    build_features(v, feats, side, 4, 4)
    one(3, 2)
    shared1 = share(0, h1, 4, CH)
    for copy in started[:3]:
        copy.wait_recv()
    build_features(v, feats, side, 0, 4)
    one(1, 4)
    for copy in ones:
        copy.wait_recv()
    e2[0] = jnp.sum(e1[...], axis=0)
    shared1.wait_recv()
    two(3, 2)
    shared2 = share(1, h2, 3, CH)
    twos = []
    for j in range(1, wide):
        copy = pltpu.make_async_remote_copy(
            src_ref=e2.at[0], dst_ref=e2.at[j], send_sem=s2.at[j], recv_sem=r2.at[j],
            device_id=seconds[j - 1], device_id_type=MESH,
        )
        copy.start()
        twos.append(copy)
    two(1, 2)
    for copy in started[3:6]:
        copy.wait_recv()
    build_features(v, feats, side, -4, 2)
    one(-3, 2)
    two(-1, 3)
    shared2.wait_recv()
    three(3, 2)
    shared3 = share(2, h3, 2, CH)
    three(1, 4)
    shared3.wait_recv()
    four(3, 2)
    shared4 = share(3, st, 1, 8)
    four(1, 3)
    shared4.wait_recv()
    for copy in twos:
        copy.wait_recv()
    finish(v, st, jnp.sum(e2[...], axis=0), cells, updated, stress_out)
    for copy in started + ones + twos:
        copy.wait_send()


def solution(mesh):
    sizes = (mesh.shape["grp"], mesh.shape["gx"], mesh.shape["gy"])
    near, wide = sizes[1] // 2, sizes[0] * 2 * sizes[2]
    n = len(halo_copies())
    bf, f32 = jnp.bfloat16, jnp.float32

    def local(velocity, w1, b1, w2, b2, w3, b3, w4):
        spec = pl.BlockSpec(memory_space=pltpu.VMEM)
        dma = pltpu.SemaphoreType.DMA
        return pl.pallas_call(
            lambda *refs: step_kernel(sizes, *refs),
            out_shape=(
                jax.ShapeDtypeStruct((3, NX, NY, NZ), f32),
                jax.ShapeDtypeStruct((6, NX, NY, NZ), f32),
            ),
            in_specs=[pl.BlockSpec(memory_space=pltpu.HBM)] * 9,
            out_specs=(spec, spec),
            scratch_shapes=[
                pltpu.VMEM((VX, VY, 3, 1, NZ), f32),
                pltpu.VMEM((3, NX, NY, NZ), f32),
                pltpu.VMEM((near, 1, NZ), f32),
                pltpu.VMEM((wide, 1, NZ), f32),
                pltpu.VMEM((81, 3, CH), bf),
                pltpu.VMEM((1, CH), f32),
                pltpu.VMEM((27 * CH, CH), bf),
                pltpu.VMEM((1, CH), f32),
                pltpu.VMEM((27 * CH, CH), bf),
                pltpu.VMEM((1, CH), f32),
                pltpu.VMEM((27, 6, CH), bf),
                pltpu.VMEM(((VX - 2) * (VY - 2) * 32, NZ), bf),
                pltpu.VMEM(((VX - 4) * (VY - 4) * CH, NZ), bf),
                pltpu.VMEM(((VX - 6) * (VY - 6) * CH, NZ), bf),
                pltpu.VMEM(((VX - 8) * (VY - 8) * CH, NZ), bf),
                pltpu.VMEM(((VX - 10) * (VY - 10) * 8, NZ), f32),
                pltpu.VMEM((CH, 288), bf),
                pltpu.VMEM((3, 3 * CH, 3 * CH), bf),
                pltpu.VMEM((3, 3 * CH, 3 * CH), bf),
                pltpu.VMEM((3, 32, 3 * CH), bf),
                pltpu.VMEM((CH, NZ), f32),
                pltpu.VMEM((CH, NZ), f32),
                pltpu.VMEM((CH, NZ), f32),
                dma((4,)),
                dma((7,)),
                dma((n,)),
                dma((n,)),
                dma((near,)),
                dma((near,)),
                dma((wide,)),
                dma((wide,)),
                dma((4,)),
                dma((4,)),
            ],
            compiler_params=pltpu.CompilerParams(
                collective_id=0, has_side_effects=True, vmem_limit_bytes=56 << 20
            ),
            name="step",
        )(
            velocity, velocity.reshape(3, NX, NY, 1, NZ),
            jnp.transpose(w1, (0, 1, 4, 2, 3)).reshape(81, 3, CH), b1.reshape(1, CH),
            w2.reshape(27 * CH, CH), b2.reshape(1, CH),
            w3.reshape(27 * CH, CH), b3.reshape(1, CH),
            w4.reshape(27, 6, CH),
        )

    block = P(None, ("grp", "gx"), "gy", None)
    return jax.shard_map(
        local,
        mesh=mesh,
        in_specs=(block,) + (P(),) * 7,
        out_specs=(block, block),
        check_vma=False,
    )
```

time: 48 us -> 40.7 us (0.85)
  Pallas kernels: 43.2 us -> 37.8 us
  local copies, waits for them, and re-layouts: 4 us -> 2.1 us
    pallas_call x1, Pallas kernels: 43.2 us -> 37.8 us  [local(): pl.pallas_call(lambda *refs: step_kernel(sizes, *refs), out_shape=(jax.Sh...]
    unnamed x5 -> x4, local copies, waits for them, and re-layouts: 4 us -> 2.1 us
where the time goes in v2:
time: 40.7 us; the launch traced here: 40.5 us
  Pallas kernels  37.8 us (93%)
  local copies, waits for them, and re-layouts  2.1 us (5%)
  between operations  0.65 us (2%)
    pallas_call x1, Pallas kernels, local(): pl.pallas_call(lambda *refs: step_kernel(sizes, *refs), out_shape=(jax.Sh...  37.8 us
    unnamed x4, local copies, waits for them, and re-layouts  2.1 us

profile of v2, /device:TPU:1, one launch (start us, length us, event | category | flops | bytes accessed | tf_op | source)
XLA Modules:
  0.0 40.5 jit_solution(11811322784166051395)
XLA Ops:
  0.6 37.8 %step.1 = (f32[3,4,8,128]{3,2,1,0:T(8,128)}, f32[6,4,8,128]{3,2,1,0:T(8,128)}) custom-call(f32[3,4,8,128]{3,2,1,0:T(8,128)} %refs_0_.1, f32[3,4,8,1,128]{4,3,2,1,0:T(1,128)} %bitcast.12, bf16[81,3,64]{2,1,0:T(4,128)(2,1)} %bitcast.13, f32[1,64]{1,0:T(1,128)} %bitcast.15, bf16[1728,64]{1,0:T(8,128)(2,1)} %bitcast.10, f32[1,64]{1,0:T(1,128)} %bitcast.16, ...), custom_call_target="tpu_custom_call" | custom-call | tf_op jit(solution)/shard_map/step/pallas_call | solution.py:409
  38.4 0.0 copy-start
  38.4 1.5 %copy.12 = f32[3,4,8,128]{3,2,1,0:T(8,128)} copy(f32[3,4,8,128]{3,2,1,0:T(8,128)} %get-tuple-element.4) | data formatting | bytes 98304
  39.9 0.0 copy-done
  39.9 0.6 %copy.13 = f32[6,4,8,128]{3,2,1,0:T(8,128)} copy(f32[6,4,8,128]{3,2,1,0:T(8,128)S(1)} %copy-done) | data formatting | bytes 196608
Async XLA Ops:
  38.4 1.5 %copy-start = (f32[6,4,8,128]{3,2,1,0:T(8,128)S(1)}, f32[6,4,8,128]{3,2,1,0:T(8,128)}, u32[]{:S(2)}) copy-start(f32[6,4,8,128]{3,2,1,0:T(8,128)} %get-tuple-element.5) | copy-start | bytes 294916

commit v3 on v2

--- a/solution.py
+++ b/solution.py
@@ -304,8 +304,9 @@
             device_id=peers[k],
             device_id_type=MESH,
         )
-        copy.start()
         started.append(copy)
+    for k in (9, 10, 6, 7, 8, 0, 1, 2):
+        started[k].start()
 
     square = own[...]
     e1[0] = jnp.sum(jnp.sum(jnp.sum(0.5 * square * square, axis=0), axis=0), axis=0, keepdims=True)
@@ -354,6 +355,8 @@
 
     for copy in started[6:11]:
         copy.wait_recv()
+    for copy in started[3:6]:
+        copy.start()
     build_features(v, feats, side, 4, 4)
     one(3, 2)
     shared1 = share(0, h1, 4, CH)

time: 40.7 us -> 39 us (0.958)
  Pallas kernels: 37.8 us -> 36.1 us
    pallas_call x1, Pallas kernels: 37.8 us -> 36.1 us  [local(): pl.pallas_call(lambda *refs: step_kernel(sizes, *refs), out_shape=(jax.Sh...]
where the time goes in v3:
time: 39 us; the launch traced here: 38.8 us
  Pallas kernels  36.1 us (93%)
  local copies, waits for them, and re-layouts  2.1 us (5%)
  between operations  0.65 us (2%)
    pallas_call x1, Pallas kernels, local(): pl.pallas_call(lambda *refs: step_kernel(sizes, *refs), out_shape=(jax.Sh...  36.1 us
    unnamed x4, local copies, waits for them, and re-layouts  2.1 us

profile of v3, /device:TPU:1, one launch (start us, length us, event | category | flops | bytes accessed | tf_op | source)
XLA Modules:
  0.0 38.8 jit_solution(16834745828491330832)
XLA Ops:
  0.6 36.1 %step.1 = (f32[3,4,8,128]{3,2,1,0:T(8,128)}, f32[6,4,8,128]{3,2,1,0:T(8,128)}) custom-call(f32[3,4,8,128]{3,2,1,0:T(8,128)} %refs_0_.1, f32[3,4,8,1,128]{4,3,2,1,0:T(1,128)} %bitcast.12, bf16[81,3,64]{2,1,0:T(4,128)(2,1)} %bitcast.13, f32[1,64]{1,0:T(1,128)} %bitcast.15, bf16[1728,64]{1,0:T(8,128)(2,1)} %bitcast.10, f32[1,64]{1,0:T(1,128)} %bitcast.16, ...), custom_call_target="tpu_custom_call" | custom-call | tf_op jit(solution)/shard_map/step/pallas_call | solution.py:412
  36.7 0.0 copy-start
  36.7 1.5 %copy.12 = f32[3,4,8,128]{3,2,1,0:T(8,128)} copy(f32[3,4,8,128]{3,2,1,0:T(8,128)} %get-tuple-element.4) | data formatting | bytes 98304
  38.2 0.0 copy-done
  38.2 0.6 %copy.13 = f32[6,4,8,128]{3,2,1,0:T(8,128)} copy(f32[6,4,8,128]{3,2,1,0:T(8,128)S(1)} %copy-done) | data formatting | bytes 196608
Async XLA Ops:
  36.7 1.5 %copy-start = (f32[6,4,8,128]{3,2,1,0:T(8,128)S(1)}, f32[6,4,8,128]{3,2,1,0:T(8,128)}, u32[]{:S(2)}) copy-start(f32[6,4,8,128]{3,2,1,0:T(8,128)} %get-tuple-element.5) | copy-start | bytes 294916

commit v4 on v3

--- a/solution.py
+++ b/solution.py
@@ -215,16 +215,16 @@
             wp4[dx, :, dy * CH : (dy + 1) * CH] = jnp.concatenate(rows, axis=0).astype(jnp.bfloat16)
 
 
-def finish(v, st, total, cells, updated, stress_out):
+def finish_kernel(cells, v, st, total, updated, stress_out):
     sy = NY + 2
-    energy = jnp.sum(total, axis=1, keepdims=True) / cells
+    energy = jnp.sum(total[...], axis=1, keepdims=True) / cells
     forcing = power_input / (2.0 * energy + 1e-06)
     for x in range(NX):
         def tau(k, ox, oy):
             return st[pl.ds(((x + 1 + ox) * sy + 1 + oy) * 8 + k, NY, stride=8), :]
 
         def vel(k, ox, oy):
-            return v[pl.ds(((x + HALO + ox) * VY + HALO + oy) * 3 + k, NY, stride=3), :]
+            return v[pl.ds((x + 1 + ox) * 32 + (1 + oy) * 3 + k, NY, stride=3), :]
 
         here = [vel(k, 0, 0) for k in range(3)]
         for k in range(6):
@@ -243,15 +243,14 @@
 
 
 def step_kernel(
-    sizes, v_ref, vrow_ref, w1_hbm, b1_hbm, w2_hbm, b2_hbm, w3_hbm, b3_hbm, w4_hbm, updated, stress_out,
+    sizes, v_ref, vrow_ref, w1_hbm, b1_hbm, w2_hbm, b2_hbm, w3_hbm, b3_hbm, w4_hbm, st, near_v, total,
     ext, own, e1, e2, w1, b1, w2, b2, w3, b3, w4,
-    feats, h1, h2, h3, st, wp1, wp2, wp3, wp4, c1, c2, c3,
+    feats, h1, h2, h3, wp1, wp2, wp3, wp4, c1, c2, c3,
     local_sem, weight_sem, send, recv, s1, r1, s2, r2, s3, r3,
 ):
     groups, gxs, gys = sizes
     near = gxs // 2
     count_x = groups * gxs
-    cells = float(NX * NY * NZ * count_x * gys)
     grp, gx, gy = lax.axis_index("grp"), lax.axis_index("gx"), lax.axis_index("gy")
     xi = grp * gxs + gx
     p = lax.rem(gx, near)
@@ -392,10 +391,14 @@
     four(3, 2)
     shared4 = share(3, st, 1, 8)
     four(1, 3)
+    for x in range(NX + 2):
+        row = ((x + HALO - 1) * VY + HALO - 1) * 3
+        for part in range(4):
+            near_v[x * 32 + part * 8 : x * 32 + part * 8 + 8, :] = v[pl.ds(row + part * 8, 8), :]
     shared4.wait_recv()
     for copy in twos:
         copy.wait_recv()
-    finish(v, st, jnp.sum(e2[...], axis=0), cells, updated, stress_out)
+    total[...] = jnp.sum(e2[...], axis=0)
     for copy in started + ones + twos:
         copy.wait_send()
 
@@ -404,19 +407,21 @@
     sizes = (mesh.shape["grp"], mesh.shape["gx"], mesh.shape["gy"])
     near, wide = sizes[1] // 2, sizes[0] * 2 * sizes[2]
     n = len(halo_copies())
+    cells = float(NX * NY * NZ * sizes[0] * sizes[1] * sizes[2])
     bf, f32 = jnp.bfloat16, jnp.float32
 
     def local(velocity, w1, b1, w2, b2, w3, b3, w4):
         spec = pl.BlockSpec(memory_space=pltpu.VMEM)
         dma = pltpu.SemaphoreType.DMA
-        return pl.pallas_call(
+        parts = pl.pallas_call(
             lambda *refs: step_kernel(sizes, *refs),
             out_shape=(
-                jax.ShapeDtypeStruct((3, NX, NY, NZ), f32),
-                jax.ShapeDtypeStruct((6, NX, NY, NZ), f32),
+                jax.ShapeDtypeStruct(((VX - 10) * (VY - 10) * 8, NZ), f32),
+                jax.ShapeDtypeStruct(((NX + 2) * 32, NZ), f32),
+                jax.ShapeDtypeStruct((1, NZ), f32),
             ),
             in_specs=[pl.BlockSpec(memory_space=pltpu.HBM)] * 9,
-            out_specs=(spec, spec),
+            out_specs=(spec, spec, spec),
             scratch_shapes=[
                 pltpu.VMEM((VX, VY, 3, 1, NZ), f32),
                 pltpu.VMEM((3, NX, NY, NZ), f32),
@@ -433,7 +438,6 @@
                 pltpu.VMEM(((VX - 4) * (VY - 4) * CH, NZ), bf),
                 pltpu.VMEM(((VX - 6) * (VY - 6) * CH, NZ), bf),
                 pltpu.VMEM(((VX - 8) * (VY - 8) * CH, NZ), bf),
-                pltpu.VMEM(((VX - 10) * (VY - 10) * 8, NZ), f32),
                 pltpu.VMEM((CH, 288), bf),
                 pltpu.VMEM((3, 3 * CH, 3 * CH), bf),
                 pltpu.VMEM((3, 3 * CH, 3 * CH), bf),
@@ -463,6 +467,17 @@
             w3.reshape(27 * CH, CH), b3.reshape(1, CH),
             w4.reshape(27, 6, CH),
         )
+        held, near_v, total = parts
+        return pl.pallas_call(
+            lambda *refs: finish_kernel(cells, *refs),
+            out_shape=(
+                jax.ShapeDtypeStruct((3, NX, NY, NZ), f32),
+                jax.ShapeDtypeStruct((6, NX, NY, NZ), f32),
+            ),
+            in_specs=[spec] * 3,
+            out_specs=(spec, spec),
+            name="finish",
+        )(near_v, held, total)
 
     block = P(None, ("grp", "gx"), "gy", None)
     return jax.shard_map(

time: 39 us -> 38.6 us (0.990)
  local copies, waits for them, and re-layouts: 2.1 us -> 0 us
  Pallas kernels: 36.1 us -> 37.8 us
    unnamed x4 -> x0, local copies, waits for them, and re-layouts: 2.1 us -> none
    pallas_call x0 -> x1, Pallas kernels: none -> 1.78 us  [local(): pl.pallas_call(lambda *refs: finish_kernel(cells, *refs), out_shape=(jax....]
where the time goes in v4:
time: 38.6 us; the launch traced here: 38.4 us
  Pallas kernels  37.8 us (98%)
  between operations  0.64 us (2%)
    pallas_call x1, Pallas kernels, local(): pl.pallas_call(lambda *refs: step_kernel(sizes, *refs), out_shape=(jax.Sh...  36 us
    pallas_call x1, Pallas kernels, local(): pl.pallas_call(lambda *refs: finish_kernel(cells, *refs), out_shape=(jax....  1.78 us

profile of v4, /device:TPU:1, one launch (start us, length us, event | category | flops | bytes accessed | tf_op | source)
XLA Modules:
  0.0 38.4 jit_solution(6014959072649089201)
XLA Ops:
  0.6 36.0 %step.1 = (f32[480,128]{1,0:T(8,128)}, f32[192,128]{1,0:T(8,128)}, f32[1,128]{1,0:T(1,128)}) custom-call(f32[3,4,8,128]{3,2,1,0:T(8,128)} %refs_0_.1, f32[3,4,8,1,128]{4,3,2,1,0:T(1,128)} %bitcast.12, bf16[81,3,64]{2,1,0:T(4,128)(2,1)} %bitcast.13, f32[1,64]{1,0:T(1,128)} %bitcast.15, bf16[1728,64]{1,0:T(8,128)(2,1)} %bitcast.10, f32[1,64]{1,0:T(1,128)} %bitcast.16, ...), custom_call_target="tpu_custom_call" | custom-call | tf_op jit(solution)/shard_map/step/pallas_call | solution.py:416
  36.7 1.8 %finish.1 = (f32[3,4,8,128]{3,2,1,0:T(8,128)}, f32[6,4,8,128]{3,2,1,0:T(8,128)}) custom-call(f32[192,128]{1,0:T(8,128)} %get-tuple-element.5.refs_0_, f32[480,128]{1,0:T(8,128)} %get-tuple-element.6.refs_1_, f32[1,128]{1,0:T(1,128)} %get-tuple-element.7.refs_2_), custom_call_target="tpu_custom_call" | custom-call | tf_op jit(solution)/shard_map/finish/pallas_call | solution.py:471

commit v5 on v4

--- a/solution.py
+++ b/solution.py
@@ -212,7 +212,7 @@
                 tap = (dx * 3 + dy) * 3 + dz
                 rows += [w4[tap].astype(jnp.float32), blank]
             rows.append(jnp.zeros((8, CH), jnp.float32))
-            wp4[dx, :, dy * CH : (dy + 1) * CH] = jnp.concatenate(rows, axis=0).astype(jnp.bfloat16)
+            wp4[dx * 32 : (dx + 1) * 32, dy * CH : (dy + 1) * CH] = jnp.concatenate(rows, axis=0).astype(jnp.bfloat16)
 
 
 def finish_kernel(cells, v, st, total, updated, stress_out):
@@ -336,7 +336,16 @@
         conv(h2, wide_taps(wp3), 2, side, high, count, hidden_emit(h3, c3, 2))
 
     def four(high, count):
-        conv(h3, wide_taps(wp4), 1, side, high, count, last_emit(st))
+        low = high - count + 1
+        first = 1 + low + side * (3 - high - low)
+        emit = last_emit(st)
+        for y in range(0, NY + 2, 2):
+            terms = [
+                dot(wp4[...], beside(lambda j: window(h3, CH, first + i, y + j, NY + 4, 3)))
+                for i in range(count + 2)
+            ]
+            for t in range(count):
+                emit(first + t, y, terms[t][:32] + terms[t + 1][32:64] + terms[t + 2][64:])
 
     def share(slot, held, halo, width):
         rows = (NY + 2 * halo) * width
@@ -441,7 +450,7 @@
                 pltpu.VMEM((CH, 288), bf),
                 pltpu.VMEM((3, 3 * CH, 3 * CH), bf),
                 pltpu.VMEM((3, 3 * CH, 3 * CH), bf),
-                pltpu.VMEM((3, 32, 3 * CH), bf),
+                pltpu.VMEM((96, 3 * CH), bf),
                 pltpu.VMEM((CH, NZ), f32),
                 pltpu.VMEM((CH, NZ), f32),
                 pltpu.VMEM((CH, NZ), f32),

time: 38.6 us -> 38.4 us (level)
  no operation moved by 1% of the time
where the time goes in v5:
time: 38.4 us; the launch traced here: 38.3 us
  Pallas kernels  37.6 us (98%)
  between operations  0.64 us (2%)
    pallas_call x1, Pallas kernels, local(): pl.pallas_call(lambda *refs: step_kernel(sizes, *refs), out_shape=(jax.Sh...  35.9 us
    pallas_call x1, Pallas kernels, local(): pl.pallas_call(lambda *refs: finish_kernel(cells, *refs), out_shape=(jax....  1.78 us

profile of v5, /device:TPU:1, one launch (start us, length us, event | category | flops | bytes accessed | tf_op | source)
XLA Modules:
  0.0 38.3 jit_solution(11624544139251660487)
XLA Ops:
  0.6 35.9 %step.1 = (f32[480,128]{1,0:T(8,128)}, f32[192,128]{1,0:T(8,128)}, f32[1,128]{1,0:T(1,128)}) custom-call(f32[3,4,8,128]{3,2,1,0:T(8,128)} %refs_0_.1, f32[3,4,8,1,128]{4,3,2,1,0:T(1,128)} %bitcast.12, bf16[81,3,64]{2,1,0:T(4,128)(2,1)} %bitcast.13, f32[1,64]{1,0:T(1,128)} %bitcast.15, bf16[1728,64]{1,0:T(8,128)(2,1)} %bitcast.10, f32[1,64]{1,0:T(1,128)} %bitcast.16, ...), custom_call_target="tpu_custom_call" | custom-call | tf_op jit(solution)/shard_map/step/pallas_call | solution.py:425
  36.5 1.8 %finish.1 = (f32[3,4,8,128]{3,2,1,0:T(8,128)}, f32[6,4,8,128]{3,2,1,0:T(8,128)}) custom-call(f32[192,128]{1,0:T(8,128)} %get-tuple-element.5.refs_0_, f32[480,128]{1,0:T(8,128)} %get-tuple-element.6.refs_1_, f32[1,128]{1,0:T(1,128)} %get-tuple-element.7.refs_2_), custom_call_target="tpu_custom_call" | custom-call | tf_op jit(solution)/shard_map/finish/pallas_call | solution.py:480
